TPU v7x, 32 devices: a whole 2x2x4 slice. The times are simulated.
32 devices in a mesh: row: 8 (over z, x), col: 4 (over y, core).
Axes of the slice: x: 2, y: 2, z: 4, core: 2. Of those that a mesh axis runs over, the one named last changes fastest.
Arguments:
- gradient: bfloat16 [3072, 14336], P('row', 'col'), may hold values from -0.1875 to 0.1875
- left_factor: float32 [3072, 3072], P('row', 'col'), may hold values from -1 to 11, as said below
- right_factor: float32 [14336, 14336], P('col', 'row'), may hold values from -1 to 3, as said below
- left_basis: bfloat16 [3072, 3072], P('row', 'col'), may hold values from -0.109375 to 0.109375
- right_basis: bfloat16 [14336, 2048], P('row', 'col'), may hold values from -0.046875 to 0.046875
Outputs:
- left_new: float32 [3072, 3072], P('row', 'col')
- right_new: float32 [14336, 14336], P('col', 'row')
- left_out: float32 [3072, 3072], P('row', 'col')
- right_out: float32 [14336, 2048], P('col', 'row')
Inputs may be any that keep to these rules, and one draw needn't show every extreme that they name: left_factor is symmetric. right_factor is symmetric.
All inputs are finite; a program needn't handle non-finite values.
Results may differ from a plain program's by a relative error of at most 0.0029.
Values may be sent and summed in bfloat16 or wider, within the bound.
A program may use at most 192 MiB of HBM per device.

v0:
```python
import jax
import jax.numpy as jnp
from jax import lax
from jax.sharding import PartitionSpec as P

DMODEL = 3072
DHIDDEN = 14336
ema_decay = 0.95
epsilon = 1e-06


def spread(block, axis, holder):
    block = jnp.where(lax.axis_index(axis) == holder, block, jnp.zeros_like(block))
    return lax.psum(block, axis)


def on_device(gradient, left_factor, right_factor, left_basis, right_basis):
    row_count = lax.axis_size("row")
    col_count = lax.axis_size("col")
    row_index = lax.axis_index("row")
    column_slab = lax.all_gather(gradient, "row", axis=0, tiled=True)
    gram_block = lax.psum_scatter(
        lax.dot_general(
            column_slab, gradient, (((1,), (1,)), ((), ())), preferred_element_type=jnp.float32
        ),
        "col",
        scatter_dimension=0,
        tiled=True,
    ).T
    left_new = ema_decay * left_factor + (1.0 - ema_decay) * gram_block
    group_ratio = row_count // col_count
    slab_cols = gradient.shape[1] // group_ratio
    offered = lax.dynamic_slice_in_dim(
        column_slab, row_index % group_ratio * slab_cols, slab_cols, 1
    )
    shared = spread(offered, "col", row_index // group_ratio)
    right_block = lax.dot_general(
        column_slab, shared, (((0,), (0,)), ((), ())), preferred_element_type=jnp.float32
    )
    right_new = ema_decay * right_factor + (1.0 - ema_decay) * right_block
    left_half = left_new.astype(jnp.bfloat16)
    left_rows = lax.all_gather(left_half, "col", axis=1, tiled=True)
    left_prod = jnp.dot(
        left_rows,
        lax.all_gather(left_basis, "row", axis=0, tiled=True),
        preferred_element_type=jnp.float32,
    )
    right_half = right_new.astype(jnp.bfloat16)
    basis_full = lax.all_gather(right_basis, "col", axis=1, tiled=True)
    right_prod = lax.psum_scatter(
        lax.dot_general(
            basis_full, right_half, (((0,), (1,)), ((), ())), preferred_element_type=jnp.float32
        ),
        "row",
        scatter_dimension=0,
        tiled=True,
    ).T
    left_sq = jnp.sum(left_prod * left_prod, axis=0)
    right_sq = jnp.sum(right_prod * right_prod, axis=0)
    left_sq = lax.psum(left_sq, "row")
    right_sq = lax.psum(right_sq, "col")
    left_out = left_prod * lax.rsqrt(left_sq / DMODEL + epsilon)
    right_out = right_prod * lax.rsqrt(right_sq / DHIDDEN + epsilon)
    return (left_new, right_new, left_out, right_out)


def solution(mesh):
    in_specs = (P("row", "col"), P("row", "col"), P("col", "row"), P("row", "col"), P("row", "col"))
    out_specs = (P("row", "col"), P("col", "row"), P("row", "col"), P("col", "row"))
    return jax.shard_map(
        on_device, mesh=mesh, in_specs=in_specs, out_specs=out_specs, check_vma=False
    )
```

profile of v0, /device:TPU:0, one launch (start us, length us, event | category | flops | bytes accessed | tf_op | source)
XLA Modules:
  0.0 1338.3 jit_solution(2984441622477216147)
XLA Ops:
  7.2 0.7 all-gather.5.cloned.1.call-update
  7.9 0.0 all-reduce.2.cloned.1.call-start
  8.0 425.7 %all-gather.5.cloned.1.call-done = bf16[3072,3584]{1,0:T(8,128)(2,1)} async-done(((bf16[384,3584]{1,0:T(8,128)(2,1)}), bf16[3072,3584]{1,0:T(8,128)(2,1)}) %all-gather.5.cloned.1.call-update) | async-done | bytes 22020112 | tf_op jit(solution)/shard_map/all_gather | solution.py:21
  433.6 10.6 dynamic-slice_select_fusion
  444.3 0.0 reduce-scatter.3.cloned.1.call-start
  444.3 1.7 copy-done
  446.0 17.8 %fusion.2 = f32[3072,384]{1,0:T(8,128)} fusion(bf16[3072,3584]{1,0:T(8,128)(2,1)} %all-gather.5.cloned.1.call-done, bf16[384,3584]{1,0:T(8,128)(2,1)S(1)} %copy-done), kind=kOutput, calls=%fused_computation.12 | convolution fusion | flops 8455716864 | bytes 29491200 | tf_op jit(solution)/shard_map/dot_general | solution.py:23
  463.8 0.0 all-gather.11.cloned.1.call-start
  463.9 0.5 all-gather.11.cloned.1.call-update
  464.5 0.5 all-gather.9.cloned.1.call-update
  465.0 0.0 all-gather.7.cloned.1.call-start
  465.0 0.1 copy-done.1
  465.1 0.4 copy.9
  465.5 27.4 %copy.10 = f32[3584,1792]{0,1:T(8,128)} copy(f32[3584,1792]{1,0:T(8,128)} %param.7) | data formatting | bytes 51380224 | tf_op args[2]
  492.9 146.8 %all-reduce.2.cloned.1.call-done = bf16[3072,1792]{1,0:T(8,128)(2,1)} async-done(((bf16[3072,1792]{1,0:T(8,128)(2,1)}), bf16[3072,1792]{1,0:T(8,128)(2,1)}) %all-reduce.2.cloned.1.call-update) | async-done | bytes 11010064 | tf_op jit(solution)/shard_map/psum | solution.py:14
  639.7 50.6 %bitcast_add_fusion = f32[3584,1792]{0,1:T(8,128)} fusion(f32[3584,1792]{0,1:T(8,128)} %copy.10, bf16[3072,1792]{1,0:T(8,128)(2,1)} %all-reduce.2.cloned.1.call-done, bf16[3072,3584]{1,0:T(8,128)(2,1)} %all-gather.5.cloned.1.call-done), kind=kOutput, calls=%fused_computation | convolution fusion | flops 39479279616 | bytes 84410368 | tf_op jit(solution)/shard_map/dot_general | solution.py:37
  690.3 0.1 reduce-scatter.3.cloned.1.call-done
  690.4 2.3 fusion.1
  692.7 0.2 reduce-scatter.5.cloned.1.call-start
  692.9 51.2 %all-gather.11.cloned.1.call-done = bf16[1792,2048]{1,0:T(8,128)(2,1)} async-done(((bf16[1792,512]{1,0:T(8,128)(2,1)}), bf16[1792,2048]{1,0:T(8,128)(2,1)}) %all-gather.11.cloned.1.call-update) | async-done | bytes 7340048 | tf_op jit(solution)/shard_map/all_gather | solution.py:49
  744.2 35.4 %convolution_bitcast_fusion = f32[2048,3584]{0,1:T(8,128)} fusion(bf16[1792,2048]{1,0:T(8,128)(2,1)} %all-gather.11.cloned.1.call-done, f32[3584,1792]{0,1:T(8,128)} %bitcast_add_fusion), kind=kOutput, calls=%fused_computation.1 | convolution fusion | flops 26313097216 | bytes 62390272 | tf_op jit(solution)/shard_map/dot_general | solution.py:51
  779.6 27.5 %copy.12 = f32[3584,1792]{1,0:T(8,128)} copy(f32[3584,1792]{0,1:T(8,128)} %bitcast_add_fusion) | data formatting | bytes 51380224
  807.1 1.4 copy.11
  808.4 17.1 %all-gather.9.cloned.1.call-done = bf16[3072,768]{1,0:T(8,128)(2,1)} async-done(((bf16[384,768]{1,0:T(8,128)(2,1)}), bf16[3072,768]{1,0:T(8,128)(2,1)}) %all-gather.9.cloned.1.call-update) | async-done | bytes 4718608 | tf_op jit(solution)/shard_map/all_gather | solution.py:45
  825.5 24.4 %all-gather.7.cloned.1.call-done = bf16[384,3072]{0,1:T(8,128)(2,1)} async-done(((bf16[384,768]{0,1:T(8,128)(2,1)}), bf16[384,3072]{0,1:T(8,128)(2,1)}) %all-gather.7.cloned.1.call-update) | async-done | bytes 2359312 | tf_op jit(solution)/shard_map/all_gather | solution.py:42
  850.0 5.1 multiply_reduce_fusion.1
  855.1 22.3 %psum.22 = f32[768]{0:T(1024)S(1)} all-reduce(f32[768]{0:T(1024)S(1)} %get-tuple-element.10), channel_id=1, replica_groups=mesh['row'=8,'col'=4] {'row'}, use_global_device_ids=true, to_apply=%region_3.4 | all-reduce | flops 768 | bytes 6144 | tf_op jit(solution)/shard_map/psum | solution.py:60
  877.4 1.1 broadcast_multiply_fusion
  878.5 439.8 %reduce-scatter.5.cloned.1.call-done = f32[256,3584]{0,1:T(8,128)} async-done(((f32[2048,3584]{0,1:T(8,128)}), f32[256,3584]{0,1:T(8,128)}) %reduce-scatter.5.cloned.1.call-update) | async-done | bytes 3670032 | tf_op jit(solution)/shard_map/reduce_scatter | solution.py:50
  1318.3 2.5 multiply_reduce_fusion
  1320.9 6.5 psum.23
  1327.4 4.1 multiply_bitcast_fusion
  (10 shorter events, 0.2 us)
Async XLA Ops:
  7.2 426.5 %all-gather.5.cloned.1.call-start = ((), (), s32[]{:S(2)}) async-start(), calls=%async_computation.2 | async-start | bytes 24772608 | tf_op jit(solution)/shard_map/all_gather | solution.py:21
  7.9 631.8 %all-reduce.2.cloned.1.call-start = ((), (), s32[]{:S(2)}) async-start(), calls=%async_computation.4 | async-start | bytes 22020096 | tf_op jit(solution)/shard_map/psum | solution.py:14
  444.3 1.8 copy-start
  444.3 246.1 %reduce-scatter.3.cloned.1.call-start = ((), (), s32[]{:S(2)}) async-start(), calls=%async_computation.3 | async-start | bytes 5898240 | tf_op jit(solution)/shard_map/reduce_scatter | solution.py:22
  463.8 1.3 copy-start.1
  463.8 280.3 %all-gather.11.cloned.1.call-start = ((), (), s32[]{:S(2)}) async-start(), calls=%async_computation.7 | async-start | bytes 9175040 | tf_op jit(solution)/shard_map/all_gather | solution.py:49
  464.4 361.1 %all-gather.9.cloned.1.call-start = ((), (), s32[]{:S(2)}) async-start(), calls=%async_computation.6 | async-start | bytes 5308416 | tf_op jit(solution)/shard_map/all_gather | solution.py:45
  465.0 385.0 %all-gather.7.cloned.1.call-start = ((), (), s32[]{:S(2)}) async-start(), calls=%async_computation.5 | async-start | bytes 2949120 | tf_op jit(solution)/shard_map/all_gather | solution.py:42
  692.7 625.6 %reduce-scatter.5.cloned.1.call-start = ((), (), s32[]{:S(2)}) async-start(), calls=%async_computation.8 | async-start | bytes 33030144 | tf_op jit(solution)/shard_map/reduce_scatter | solution.py:50
Sparse Core Ops, SparseCore 0:
  9.5 424.0 all-gather.4
  444.4 195.1 all-reduce.1
  642.2 48.1 reduce-scatter.2
  691.8 52.2 all-gather.10
  746.2 79.3 all-gather.8
  827.5 22.4 all-gather.6
  853.9 464.4 reduce-scatter.4
where the time goes:
time: 1340 us
  waiting for transfers between devices  1110 us (83%)
  matrix products  109 us (8%)
  local copies, waits for them, and re-layouts  58.4 us (4%)
  blocking collectives  28.8 us (2%)
  other arithmetic  20.7 us (2%)
  between operations  14.2 us (1%)
    reduce_scatter x1, waiting for transfers between devices, on_device(): lax.psum_scatter(lax.dot_general(basis_full, right_half, (((0,), (1,)), (...  440 us
    all_gather x1, waiting for transfers between devices, on_device(): column_slab = lax.all_gather(gradient, 'row', axis=0, tiled=True)  426 us
    psum x1, waiting for transfers between devices, spread(): return lax.psum(block, axis)  147 us
    unnamed x8, local copies, waits for them, and re-layouts  58.4 us
    all_gather x1, waiting for transfers between devices, on_device(): basis_full = lax.all_gather(right_basis, 'col', axis=1, tiled=True)  51.2 us
    dot_general x1, matrix products, on_device(): lax.dot_general(column_slab, shared, (((0,), (0,)), ((), ())), preferred_...  50.6 us
    dot_general x1, matrix products, on_device(): lax.dot_general(basis_full, right_half, (((0,), (1,)), ((), ())), preferr...  35.4 us
  transfers between devices with their start and end apart: 7, of which 7 were waited for; matrix products, arithmetic and copies ran while one was open for 13% of the time, Pallas kernels for 0%

commit v1 on v0

--- a/solution.py
+++ b/solution.py
@@ -11,7 +11,7 @@
 
 def spread(block, axis, holder):
     block = jnp.where(lax.axis_index(axis) == holder, block, jnp.zeros_like(block))
-    return lax.psum(block, axis)
+    return jnp.sum(lax.all_gather(block, axis), axis=0)
 
 
 def on_device(gradient, left_factor, right_factor, left_basis, right_basis):

time: 1340 us -> 1410 us (1.052)
  waiting for transfers between devices: 1110 us -> 1160 us
  other arithmetic: 20.7 us -> 44.5 us
    all_gather x0 -> x1, waiting for transfers between devices: none -> 261 us  [spread(): return jnp.sum(lax.all_gather(block, axis), axis=0)]
    psum x1 -> x0, waiting for transfers between devices: 147 us -> none  [spread(): return lax.psum(block, axis)]
    all_gather x1, waiting for transfers between devices: 51.2 us -> 0.01 us  [on_device(): basis_full = lax.all_gather(right_basis, 'col', axis=1, tiled=True)]
    reduce_scatter x1, waiting for transfers between devices: 440 us -> 412 us  [on_device(): lax.psum_scatter(lax.dot_general(basis_full, right_half, (((0,), (1,)), (...]
    reduce_sum x0 -> x1, other arithmetic: none -> 23.6 us  [spread(): return jnp.sum(lax.all_gather(block, axis), axis=0)]
    unnamed x8 -> x6, local copies, waits for them, and re-layouts: 58.4 us -> 56.3 us
  transfers between devices with their start and end apart: 7 -> 7, of which waited for: 7 -> 6; matrix products, arithmetic and copies ran while one was open for 13% -> 13% of each run, Pallas kernels for 0% -> 0%
where the time goes in v1:
time: 1410 us
  waiting for transfers between devices  1160 us (82%)
  matrix products  110 us (8%)
  local copies, waits for them, and re-layouts  56.3 us (4%)
  other arithmetic  44.5 us (3%)
  blocking collectives  28.8 us (2%)
  between operations  14.2 us (1%)
    all_gather x1, waiting for transfers between devices, on_device(): column_slab = lax.all_gather(gradient, 'row', axis=0, tiled=True)  426 us
    reduce_scatter x1, waiting for transfers between devices, on_device(): lax.psum_scatter(lax.dot_general(basis_full, right_half, (((0,), (1,)), (...  412 us
    all_gather x1, waiting for transfers between devices, spread(): return jnp.sum(lax.all_gather(block, axis), axis=0)  261 us
    unnamed x6, local copies, waits for them, and re-layouts  56.3 us
    dot_general x1, matrix products, on_device(): lax.dot_general(column_slab, shared, (((0,), (0,)), ((), ())), preferred_...  50.7 us
    dot_general x1, matrix products, on_device(): lax.dot_general(basis_full, right_half, (((0,), (1,)), ((), ())), preferr...  35.8 us
  transfers between devices with their start and end apart: 7, of which 6 were waited for; matrix products, arithmetic and copies ran while one was open for 13% of the time, Pallas kernels for 0%

profile of v1, /device:TPU:0, one launch (start us, length us, event | category | flops | bytes accessed | tf_op | source)
XLA Modules:
  0.0 1411.5 jit_solution(7311706112952049943)
XLA Ops:
  7.2 0.0 all-gather.7.cloned.1.call-start
  7.2 0.7 all-gather.7.cloned.1.call-update
  7.9 0.0 reduce-scatter.3.cloned.1.call-start
  7.9 425.7 %all-gather.7.cloned.1.call-done = bf16[3072,3584]{1,0:T(8,128)(2,1)} async-done(((bf16[384,3584]{1,0:T(8,128)(2,1)}), bf16[3072,3584]{1,0:T(8,128)(2,1)}) %all-gather.7.cloned.1.call-update) | async-done | bytes 22020112 | tf_op jit(solution)/shard_map/all_gather | solution.py:21
  433.6 18.1 %fusion.2 = f32[3072,384]{1,0:T(8,128)} fusion(bf16[3072,3584]{1,0:T(8,128)(2,1)} %all-gather.7.cloned.1.call-done, bf16[384,3584]{1,0:T(8,128)(2,1)} %param.5), kind=kOutput, calls=%fused_computation.12 | convolution fusion | flops 8455716864 | bytes 29491200 | tf_op jit(solution)/shard_map/dot_general | solution.py:23
  451.8 0.0 all-gather.15.cloned.1.call-start
  451.9 10.9 dynamic-slice_select_fusion
  462.8 0.0 all-gather.13.cloned.1.call-start
  462.9 0.5 all-gather.13.cloned.1.call-update
  463.4 0.0 all-gather.11.cloned.1.call-start
  463.4 0.5 all-gather.11.cloned.1.call-update
  464.0 0.0 all-gather.9.cloned.1.call-start
  464.0 27.2 %copy.10 = f32[3584,1792]{0,1:T(8,128)} copy(f32[3584,1792]{1,0:T(8,128)} %param.7) | data formatting | bytes 51380224 | tf_op args[2]
  491.2 0.4 copy.9
  491.6 8.3 reduce-scatter.3.cloned.1.call-done
  499.9 2.3 fusion.1
  502.2 0.2 reduce-scatter.5.cloned.1.call-start
  502.4 261.1 %all-gather.15.cloned.1.call-done = bf16[12288,1792]{1,0:T(8,128)(2,1)} async-done(((bf16[3072,1792]{1,0:T(8,128)(2,1)}), bf16[12288,1792]{1,0:T(8,128)(2,1)}) %all-gather.15.cloned.1.call-update) | async-done | bytes 44040208 | tf_op jit(solution)/shard_map/all_gather | solution.py:14
  763.5 23.6 %reduce_sum.30 = bf16[3072,1792]{1,0:T(8,128)(2,1)} reduce(bf16[4,3072,1792]{2,1,0:T(8,128)(2,1)} %bitcast.17, bf16[]{:T(256)} %constant.53.clone.1), dimensions={0}, to_apply=%region_1.2 | reduce | flops 16515072 | bytes 55050240 | tf_op jit(solution)/shard_map/reduce_sum | solution.py:14
  787.1 50.7 %bitcast_add_fusion = f32[3584,1792]{0,1:T(8,128)} fusion(f32[3584,1792]{0,1:T(8,128)} %copy.10, bf16[3072,1792]{1,0:T(8,128)(2,1)} %reduce_sum.30, bf16[3072,3584]{1,0:T(8,128)(2,1)} %all-gather.7.cloned.1.call-done), kind=kOutput, calls=%fused_computation | convolution fusion | flops 39479279616 | bytes 84410368 | tf_op jit(solution)/shard_map/dot_general | solution.py:37
  837.8 35.8 %convolution_bitcast_fusion = f32[2048,3584]{0,1:T(8,128)} fusion(bf16[1792,2048]{1,0:T(8,128)(2,1)} %all-gather.13.cloned.1.call-done, f32[3584,1792]{0,1:T(8,128)} %bitcast_add_fusion), kind=kOutput, calls=%fused_computation.1 | convolution fusion | flops 26313097216 | bytes 62390272 | tf_op jit(solution)/shard_map/dot_general | solution.py:51
  873.6 1.4 copy.11
  874.9 23.7 %all-gather.11.cloned.1.call-done = bf16[3072,768]{1,0:T(8,128)(2,1)} async-done(((bf16[384,768]{1,0:T(8,128)(2,1)}), bf16[3072,768]{1,0:T(8,128)(2,1)}) %all-gather.11.cloned.1.call-update) | async-done | bytes 4718608 | tf_op jit(solution)/shard_map/all_gather | solution.py:45
  898.6 24.5 %all-gather.9.cloned.1.call-done = bf16[384,3072]{0,1:T(8,128)(2,1)} async-done(((bf16[384,768]{0,1:T(8,128)(2,1)}), bf16[384,3072]{0,1:T(8,128)(2,1)}) %all-gather.9.cloned.1.call-update) | async-done | bytes 2359312 | tf_op jit(solution)/shard_map/all_gather | solution.py:42
  923.1 5.1 multiply_reduce_fusion.1
  928.2 22.3 %psum.14 = f32[768]{0:T(1024)S(1)} all-reduce(f32[768]{0:T(1024)S(1)} %get-tuple-element.10), channel_id=1, replica_groups=mesh['row'=8,'col'=4] {'row'}, use_global_device_ids=true, to_apply=%region_3.4 | all-reduce | flops 768 | bytes 6144 | tf_op jit(solution)/shard_map/psum | solution.py:60
  950.5 1.1 broadcast_multiply_fusion
  951.6 27.4 %copy.12 = f32[3584,1792]{1,0:T(8,128)} copy(f32[3584,1792]{0,1:T(8,128)} %bitcast_add_fusion) | data formatting | bytes 51380224
  979.1 412.4 %reduce-scatter.5.cloned.1.call-done = f32[256,3584]{0,1:T(8,128)} async-done(((f32[2048,3584]{0,1:T(8,128)}), f32[256,3584]{0,1:T(8,128)}) %reduce-scatter.5.cloned.1.call-update) | async-done | bytes 3670032 | tf_op jit(solution)/shard_map/reduce_scatter | solution.py:50
  1391.5 2.5 multiply_reduce_fusion
  1394.0 6.5 psum.15
  1400.5 4.1 multiply_bitcast_fusion
  (9 shorter events, 0.1 us)
Async XLA Ops:
  7.2 426.5 %all-gather.7.cloned.1.call-start = ((), (), s32[]{:S(2)}) async-start(), calls=%async_computation.2 | async-start | bytes 24772608 | tf_op jit(solution)/shard_map/all_gather | solution.py:21
  7.9 492.0 %reduce-scatter.3.cloned.1.call-start = ((), (), s32[]{:S(2)}) async-start(), calls=%async_computation.3 | async-start | bytes 5898240 | tf_op jit(solution)/shard_map/reduce_scatter | solution.py:22
  451.8 311.7 %all-gather.15.cloned.1.call-start = ((), (), s32[]{:S(2)}) async-start(), calls=%async_computation.8 | async-start | bytes 55050240 | tf_op jit(solution)/shard_map/all_gather | solution.py:14
  462.8 374.9 %all-gather.13.cloned.1.call-start = ((), (), s32[]{:S(2)}) async-start(), calls=%async_computation.6 | async-start | bytes 9175040 | tf_op jit(solution)/shard_map/all_gather | solution.py:49
  463.4 435.2 %all-gather.11.cloned.1.call-start = ((), (), s32[]{:S(2)}) async-start(), calls=%async_computation.5 | async-start | bytes 5308416 | tf_op jit(solution)/shard_map/all_gather | solution.py:45
  464.0 27.2 %copy-start = (f32[384,768]{1,0:T(8,128)S(1)}, f32[384,768]{1,0:T(8,128)}, u32[]{:S(2)}) copy-start(f32[384,768]{1,0:T(8,128)} %param.6) | copy-start | bytes 3538948
  464.0 459.1 %all-gather.9.cloned.1.call-start = ((), (), s32[]{:S(2)}) async-start(), calls=%async_computation.4 | async-start | bytes 2949120 | tf_op jit(solution)/shard_map/all_gather | solution.py:42
  502.2 889.3 %reduce-scatter.5.cloned.1.call-start = ((), (), s32[]{:S(2)}) async-start(), calls=%async_computation.7 | async-start | bytes 33030144 | tf_op jit(solution)/shard_map/reduce_scatter | solution.py:50
Sparse Core Ops, SparseCore 0:
  9.5 424.0 all-gather.6
  451.9 47.9 reduce-scatter.2
  501.5 261.9 all-gather.14
  764.9 52.2 all-gather.12
  819.3 79.3 all-gather.10
  900.6 22.4 all-gather.8
  927.0 464.4 reduce-scatter.4
